TPU v7x, 32 devices: a whole 2x2x4 slice. The times are simulated.
32 devices in a mesh: col: 16 (over z, y, x), sec: 2 (over core).
Axes of the slice: x: 2, y: 2, z: 4, core: 2. Of those that a mesh axis runs over, the one named last changes fastest.
Arguments:
- mps: bfloat16 [16, 96, 6, 6, 96], P('col', 'sec'), may hold values from -6 to 6
- ket: bfloat16 [16, 6, 6, 6, 6, 2], P('col'), may hold values from -6 to 6
- left_proj: bfloat16 [16, 96, 96, 6, 6], P('col', 'sec'), may hold values from -0.109375 to 0.109375
- right_proj: bfloat16 [16, 96, 6, 6, 96], P('col', None, None, None, 'sec'), may hold values from -0.109375 to 0.109375
- bond_charge: int32 [16, 96], P('col'), may hold values from 0 to 5
- new_charge: int32 [16, 96], P('col'), may hold values from 0 to 5
- link_charge: int32 [16, 6], P('col'), may hold values from 0 to 2
- vert_charge: int32 [16, 2, 6], P('col'), may hold values from 0 to 2
Outputs:
- new_mps: bfloat16 [16, 96, 6, 6, 96], P('col', 'sec')
- log_norm: float32 [], replicated
All inputs are finite; a program needn't handle non-finite values.
Results may differ from a plain program's by a relative error of at most 0.0064.
Values may be sent and summed in bfloat16 or wider, within the bound.
A program may use at most 192 MiB of HBM per device.

v0:
```python
import jax
import jax.numpy as jnp
from jax import lax
from jax.sharding import PartitionSpec as P


def from_behind(x, axis, by):
    count = lax.axis_size(axis)
    return lax.ppermute(x, axis, [(i, (i + by) % count) for i in range(count)])


def absorb(
    mps_site,
    ket_site,
    left_site,
    right_site,
    charge_here,
    charge_next,
    fresh_here,
    fresh_next,
    link_here,
    link_next,
    vertical,
):
    upper = vertical[0]
    lower = vertical[1]
    physical = jnp.arange(ket_site.shape[4], dtype=jnp.int32)
    keep_mps = (
        charge_here[:, None, None, None] + upper[None, :, None, None] - upper[None, None, :, None]
        == charge_next[None, None, None, :]
    )
    masked_mps = jnp.where(keep_mps, mps_site, jnp.zeros_like(mps_site))
    keep_ket = (
        upper[:, None, None, None, None] + link_here[None, :, None, None, None]
        == lower[None, None, :, None, None]
        + link_next[None, None, None, :, None]
        + physical[None, None, None, None, :]
    )
    masked_ket = jnp.where(keep_ket, ket_site, jnp.zeros_like(ket_site))
    keep_left = (
        fresh_here[:, None, None, None]
        == charge_here[None, :, None, None]
        + link_here[None, None, :, None]
        - link_here[None, None, None, :]
    )
    masked_left = jnp.where(keep_left, left_site, jnp.zeros_like(left_site))
    keep_right = (
        charge_next[:, None, None, None]
        + link_next[None, :, None, None]
        - link_next[None, None, :, None]
        == fresh_next[None, None, None, :]
    )
    masked_right = jnp.where(keep_right, right_site, jnp.zeros_like(right_site))
    first = jnp.einsum(
        "xalm,auvb->xlmuvb", masked_left, masked_mps, preferred_element_type=jnp.float32
    ).astype(jnp.bfloat16)
    second = jnp.einsum(
        "xlmuvb,uldrp->xmvbdrp", first, masked_ket, preferred_element_type=jnp.float32
    ).astype(jnp.bfloat16)
    third = jnp.einsum(
        "xmvbdrp,vmesp->xbdres", second, masked_ket, preferred_element_type=jnp.float32
    ).astype(jnp.bfloat16)
    return jnp.einsum("xbdres,brsy->xdey", third, masked_right, preferred_element_type=jnp.float32)


def local(mps, ket, left_proj, right_proj, bond_charge, new_charge, link_charge, vert_charge):
    sites_here = mps.shape[0]
    half = left_proj.shape[1]
    full_mps = lax.all_gather(mps, "sec", axis=1, tiled=True)
    chi_full = full_mps.shape[1]
    legs = full_mps.shape[2]
    received = from_behind((bond_charge, new_charge, link_charge), "col", -1)
    bond_next = jnp.concatenate([bond_charge[1:], received[0]], axis=0)
    fresh_next = jnp.concatenate([new_charge[1:], received[1]], axis=0)
    link_next = jnp.concatenate([link_charge[1:], received[2]], axis=0)
    arrived = from_behind(right_proj, "col", -1)
    partial_next = jnp.concatenate([right_proj[1:], arrived], axis=0)
    right_next = lax.all_gather(partial_next, "sec", axis=4, tiled=True)
    offset = lax.axis_index("sec") * half
    fresh_half = lax.dynamic_slice_in_dim(new_charge[0], offset, half, 0)
    images = [
        absorb(
            full_mps[0],
            ket[0],
            left_proj[0],
            right_next[0],
            bond_charge[0],
            bond_next[0],
            fresh_half,
            fresh_next[0],
            link_charge[0],
            link_next[0],
            vert_charge[0],
        )
    ]
    image = jnp.stack(images, axis=0)
    partial_value = jnp.sum(image * image, axis=(1, 2, 3, 4))
    count = chi_full * legs * legs * chi_full
    columns = lax.axis_size("col")
    squares = lax.psum(partial_value, "sec")
    meansq = squares / count
    logs = 0.5 * jnp.log(meansq + 1e-06)
    total = lax.psum(jnp.sum(logs), "col")
    log_norm = total / (sites_here * columns)
    scale = lax.rsqrt(meansq + 1e-06)
    new_mps = (image * scale[:, None, None, None, None]).astype(jnp.bfloat16)
    return (new_mps, log_norm)


def solution(mesh):
    placed = (
        P("col", "sec", None, None, None),
        P("col", None, None, None, None, None),
        P("col", "sec", None, None, None),
        P("col", None, None, None, "sec"),
        P("col", None),
        P("col", None),
        P("col", None),
        P("col", None, None),
    )
    return jax.shard_map(
        local,
        mesh=mesh,
        in_specs=placed,
        out_specs=(P("col", "sec", None, None, None), P()),
        check_vma=False,
    )
```

profile of v0, /device:TPU:0, one launch (start us, length us, event | category | flops | bytes accessed | tf_op | source)
XLA Modules:
  0.0 157.0 jit_solution(7892534754930286098)
XLA Ops:
  0.6 7.0 %collective-permute-start = (s32[1,96]{1,0:T(1,128)}, s32[1,96]{1,0:T(1,128)S(1)}, u32[]{:S(2)}, u32[]{:S(2)}) collective-permute-start(s32[1,96]{1,0:T(1,128)} %param.12), channel_id=1, source_target_pairs={{0,30},{2,0},{4,2},{6,4},{8,6},{10,8},{12,10},{14,12},{16,14},{18,... | collective-permute-start | bytes 1160 | tf_op jit(solution)/shard_map/ppermute | solution.py:9
  7.6 0.5 collective-permute-start.1
  8.2 1.4 collective-permute-start.3
  9.6 0.5 collective-permute-start.2
  10.1 0.8 slice_bitcast_fusion
  10.9 0.7 broadcast_add_fusion.2
  11.6 0.7 broadcast_add_fusion.4
  12.4 0.1 broadcast_subtract_fusion.1
  12.4 0.7 broadcast_subtract_fusion.2
  13.2 0.7 dynamic-slice_bitcast_fusion
  13.9 2.6 %all_gather.6 = bf16[1,96,6,6,96]{4,1,3,2,0:T(8,128)(2,1)S(1)} all-gather(bf16[1,48,6,6,96]{4,1,3,2,0:T(8,128)(2,1)} %param.8), channel_id=1, replica_groups=mesh['col'=16,'sec'=2] {'sec'}, dimensions={1}, use_global_device_ids=true | all-gather | bytes 995328 | tf_op jit(solution)/shard_map/all_gather | solution.py:69
  16.5 0.0 collective-permute-done.1
  16.5 0.1 broadcast_add_fusion.1
  16.6 1.1 fusion.30
  17.8 0.0 collective-permute-done
  17.8 5.7 %convert_bitcast_fusion = bf16[48,6,6,6,6,96,1,1]{5,0,4,3,2,1,7,6:T(8,128)(2,1)S(1)} fusion(bf16[1,96,6,6,96]{4,1,3,2,0:T(8,128)(2,1)S(1)} %all_gather.6, s32[96]{0:T(128)S(1)} %bitcast.70, s32[96,6,6]{0,2,1:T(8,128)S(1)} %broadcast_subtract_fusion.1, bf16[1,48,96,6,6]{2,1,4,3,0:T(8,128)(2,1)} %param.10, s32[96,6,6]{0,2,1:T(8,128)S(1)} %broadcast_subtract_fusion.2, ...), kind=kOutput, calls=%fused_computation.8 | convolution fusion | flops 1153585152 | bytes 12967488 | tf_op jit(solution)/shard_map/xalm,auvb->xlmuvb/dot_general | solution.py:54
  23.4 28.1 %fusion = bf16[48,6,6,96,6,6,2,1]{3,5,6,4,2,1,0,7:T(8,128)(2,1)} fusion(bf16[48,6,6,6,6,96,1,1]{5,0,4,3,2,1,7,6:T(8,128)(2,1)S(1)} %convert_bitcast_fusion, bf16[6,6,6,6,2,1,1,1]{3,4,2,1,0,7,6,5:T(2,128)(2,1)S(1)} %fusion.30), kind=kOutput, calls=%fused_computation.1 | convolution fusion | flops 871907328 | bytes 35836992 | tf_op jit(solution)/shard_map/xlmuvb,uldrp->xmvbdrp/dot_general | solution.py:57
  51.5 38.6 %bitcast_convert_fusion.1 = bf16[48,96,6,6,6,6]{1,5,4,3,2,0:T(8,128)(2,1)} fusion(bf16[48,6,6,96,6,6,2,1]{3,5,6,4,2,1,0,7:T(8,128)(2,1)} %fusion, bf16[6,6,6,6,2,1,1,1]{3,4,2,1,0,7,6,5:T(2,128)(2,1)S(1)} %fusion.30), kind=kOutput, calls=%fused_computation.2 | convolution fusion | flops 865935360 | bytes 35836992 | tf_op jit(solution)/shard_map/xmvbdrp,vmesp->xbdres/dot_general | solution.py:60
  90.1 0.1 broadcast_add_fusion
  90.2 0.1 broadcast_subtract_fusion
  90.2 0.0 collective-permute-done.3
  90.2 2.8 %all_gather.7 = bf16[1,96,6,6,96]{1,4,3,2,0:T(8,128)(2,1)S(1)} all-gather(bf16[1,96,6,6,48]{1,4,3,2,0:T(8,128)(2,1)} %collective-permute-done.3), channel_id=1, replica_groups=mesh['col'=16,'sec'=2] {'sec'}, dimensions={4}, use_global_device_ids=true | all-gather | bytes 995328 | tf_op jit(solution)/shard_map/all_gather | solution.py:78
  93.0 0.0 collective-permute-done.2
  93.1 17.4 %multiply_reduce_fusion = (f32[]{:T(128)}, f32[48,6,6,96]{3,0,2,1:T(8,128)S(1)}) fusion(bf16[1,96,6,6,96]{1,4,3,2,0:T(8,128)(2,1)S(1)} %all_gather.7, s32[96,6,6]{0,2,1:T(8,128)S(1)} %broadcast_subtract_fusion, s32[96]{0:T(128)S(1)} %bitcast.73, bf16[48,96,6,6,6,6]{1,5,4,3,2,0:T(8,128)(2,1)} %bitcast_convert_fusion.1), kind=kOutput, calls=%fused_computation.16 | convolution fusion | flops 1147613184 | bytes 13285252 | tf_op jit(solution)/shard_map/xbdres,brsy->xdey/dot_general | solution.py:63
  110.4 3.1 %psum.14 = f32[1]{0:T(128)} all-reduce(f32[1]{0:T(128)} %bitcast.28), channel_id=1, replica_groups=mesh['col'=16,'sec'=2] {'sec'}, use_global_device_ids=true, to_apply=%region_1.2 | all-reduce | flops 1 | bytes 8 | tf_op jit(solution)/shard_map/psum | solution.py:100
  114.2 40.1 %psum.15 = f32[]{:T(128)} all-reduce(f32[]{:T(128)} %bitcast.31), channel_id=1, replica_groups=mesh['col'=16,'sec'=2] {'col'}, use_global_device_ids=true, to_apply=%region_2.3 | all-reduce | flops 1 | bytes 8 | tf_op jit(solution)/shard_map/psum | solution.py:103
  154.3 0.8 fusion.22
  (1 shorter events, 0.0 us)
Async XLA Ops:
  0.6 17.1 %collective-permute-start = (s32[1,96]{1,0:T(1,128)}, s32[1,96]{1,0:T(1,128)S(1)}, u32[]{:S(2)}, u32[]{:S(2)}) collective-permute-start(s32[1,96]{1,0:T(1,128)} %param.12), channel_id=1, source_target_pairs={{0,30},{2,0},{4,2},{6,4},{8,6},{10,8},{12,10},{14,12},{16,14},{18,... | collective-permute-start | bytes 1160 | tf_op jit(solution)/shard_map/ppermute | solution.py:9
  7.6 8.9 %collective-permute-start.1 = (s32[1,6]{1,0:T(1,128)}, s32[1,6]{1,0:T(1,128)S(1)}, u32[]{:S(2)}, u32[]{:S(2)}) collective-permute-start(s32[1,6]{1,0:T(1,128)} %param.14), channel_id=1, source_target_pairs={{0,30},{2,0},{4,2},{6,4},{8,6},{10,8},{12,10},{14,12},{16,14},{18,... | collective-permute-start | bytes 80 | tf_op jit(solution)/shard_map/ppermute | solution.py:9
  8.2 82.0 %collective-permute-start.3 = (bf16[1,96,6,6,48]{1,4,3,2,0:T(8,128)(2,1)}, bf16[1,96,6,6,48]{1,4,3,2,0:T(8,128)(2,1)}, u32[]{:S(2)}, u32[]{:S(2)}) collective-permute-start(bf16[1,96,6,6,48]{1,4,3,2,0:T(8,128)(2,1)} %param.11), channel_id=1, source_target_pairs={{0,30},{2,0},{4,2},{6,4},{8,6},{10,8},{12,10},{14,12},{16,14},{18,... | collective-permute-start | bytes 995336 | tf_op jit(solution)/shard_map/ppermute | solution.py:9
  9.6 83.4 %collective-permute-start.2 = (s32[1,96]{1,0:T(1,128)}, s32[1,96]{1,0:T(1,128)S(1)}, u32[]{:S(2)}, u32[]{:S(2)}) collective-permute-start(s32[1,96]{1,0:T(1,128)} %param.13), channel_id=1, source_target_pairs={{0,30},{2,0},{4,2},{6,4},{8,6},{10,8},{12,10},{14,12},{16,14},{18,... | collective-permute-start | bytes 1160 | tf_op jit(solution)/shard_map/ppermute | solution.py:9
where the time goes:
time: 157 us
  matrix products  89.7 us (57%)
  blocking collectives  48.6 us (31%)
  starting transfers between devices  9.52 us (6%)
  other arithmetic  4.45 us (3%)
  between operations  3.22 us (2%)
    psum x1, blocking collectives, local(): total = lax.psum(jnp.sum(logs), 'col')  40.1 us
    dot_general x1, matrix products, absorb(): jnp.einsum('xmvbdrp,vmesp->xbdres', second, masked_ket, preferred_element...  38.6 us
    dot_general x1, matrix products, absorb(): jnp.einsum('xlmuvb,uldrp->xmvbdrp', first, masked_ket, preferred_element_...  28.1 us
    dot_general x1, matrix products, absorb(): jnp.einsum('xbdres,brsy->xdey', third, masked_right, preferred_element_ty...  17.4 us
    ppermute x4, starting transfers between devices, from_behind(): return lax.ppermute(x, axis, [(i, (i + by) % count) for i in range(count)])  9.52 us
    dot_general x1, matrix products, absorb(): jnp.einsum('xalm,auvb->xlmuvb', masked_left, masked_mps, preferred_elemen...  5.67 us
  transfers between devices with their start and end apart: 4, of which 0 were waited for; matrix products, arithmetic and copies ran while one was open for 49% of the time, Pallas kernels for 0%

commit v1 on v0

v1 whole, which is shorter than its diff:
```python
import functools

import jax
import jax.numpy as jnp
from jax import lax
from jax.experimental import pallas as pl
from jax.experimental.pallas import tpu as pltpu
from jax.sharding import PartitionSpec as P

LANES = 128
PACK = 8
F32 = jnp.float32
BF16 = jnp.bfloat16


def from_behind(x, axis, by):
    count = lax.axis_size(axis)
    return lax.ppermute(x, axis, [(i, (i + by) % count) for i in range(count)])


def chain(legs, block, left_ref, mps_ref, up_ref, down_ref, right_ref, out_ref, sq_ref, mps_s, w1, w2, w3):
    pairs = legs // 2
    rows = legs * PACK
    wide = block * LANES

    @pl.when(pl.program_id(0) == 0)
    def _():
        for uv in range(legs * legs):
            mps_s[:, uv * LANES : (uv + 1) * LANES] = mps_ref[uv]
        sq_ref[...] = jnp.zeros_like(sq_ref)

    for u in range(legs):
        for vp in range(pairs):
            at = (u * legs + 2 * vp) * LANES
            part = jnp.dot(left_ref[...], mps_s[:, at : at + 2 * LANES], preferred_element_type=F32).astype(BF16)
            for x in range(block):
                for mp in range(pairs):
                    lo = x * rows + mp * 2 * PACK
                    for v2 in range(2):
                        w1[vp, mp, v2 * legs + u, :, x * LANES : (x + 1) * LANES] = part[
                            lo : lo + 2 * PACK, v2 * LANES : (v2 + 1) * LANES
                        ]

    slab = w2.shape[2]

    def second(i, _):
        rhs = w1[i // pairs, i % pairs].reshape(2 * legs * 2 * PACK, wide)
        part = jnp.dot(up_ref[...], rhs, preferred_element_type=F32).astype(BF16)
        w2[:, i] = part.reshape(pairs * legs, slab, wide)
        return 0

    lax.fori_loop(0, pairs * pairs, second, 0)

    for dp in range(pairs):
        for r in range(legs):
            rhs = w2[dp * legs + r].reshape(pairs * pairs * slab, wide)
            part = jnp.dot(down_ref[...], rhs, preferred_element_type=F32).astype(BF16)
            for x in range(block):
                for s in range(legs):
                    lane = (r * legs + s) * LANES
                    row = x * rows + dp * 2 * PACK
                    w3[row : row + 2 * PACK, lane : lane + LANES] = part[
                        s * 2 * PACK : (s + 1) * 2 * PACK, x * LANES : (x + 1) * LANES
                    ]

    image = jnp.dot(w3[...], right_ref[...], preferred_element_type=F32)
    out_ref[...] = image
    sq_ref[...] += jnp.sum((image * image).reshape(block * rows // 8, 8, image.shape[1]), axis=0)


def local(mps, ket, left_proj, right_proj, bond_charge, new_charge, link_charge, vert_charge):
    half = left_proj.shape[1]
    full_mps = lax.all_gather(mps, "sec", axis=1, tiled=True)[0]
    chi = full_mps.shape[0]
    legs = full_mps.shape[1]
    phys = ket.shape[5]
    pairs = legs // 2
    rows = legs * PACK
    charges = jnp.concatenate([bond_charge, new_charge, link_charge], axis=1)
    got = from_behind(charges, "col", -1)[0]
    arrived = from_behind(right_proj, "col", -1)
    right = lax.all_gather(arrived, "sec", axis=4, tiled=True)[0]
    q_here = bond_charge[0]
    q_next = got[:chi]
    n_next = got[chi : 2 * chi]
    h_next = got[2 * chi :]
    h_here = link_charge[0]
    n_half = lax.dynamic_slice_in_dim(new_charge[0], lax.axis_index("sec") * half, half, 0)
    upper, lower = vert_charge[0, 0], vert_charge[0, 1]

    keep = (
        q_here[None, None, :, None] + upper[:, None, None, None] - upper[None, :, None, None]
        == q_next[None, None, None, :]
    )
    ms = jnp.where(keep, full_mps.transpose(1, 2, 0, 3), 0).reshape(legs * legs, chi, chi)
    ms = jnp.pad(ms, ((0, 0), (0, 0), (0, LANES - chi)))
    keep = (
        n_half[:, None, None, None]
        == q_here[None, None, None, :] + h_here[None, None, :, None] - h_here[None, :, None, None]
    )
    lp = jnp.where(keep, left_proj[0].transpose(0, 3, 2, 1), 0)
    lp = jnp.pad(lp, ((0, 0), (0, 0), (0, PACK - legs), (0, 0))).reshape(half * rows, chi)
    keep = (
        q_next[None, None, :, None] + h_next[:, None, None, None] - h_next[None, :, None, None]
        == n_next[None, None, None, :]
    )
    rp = jnp.where(keep, right.transpose(1, 2, 0, 3), 0)
    rp = jnp.pad(rp, ((0, 0), (0, 0), (0, LANES - chi), (0, 0))).reshape(legs * legs * LANES, chi)
    physical = jnp.arange(phys, dtype=jnp.int32)
    keep = (
        upper[:, None, None, None, None] + h_here[None, :, None, None, None]
        == lower[None, None, :, None, None] + h_next[None, None, None, :, None] + physical
    )
    ks = jnp.where(keep, ket[0], 0)
    ks8 = jnp.pad(ks, ((0, 0), (0, PACK - legs), (0, 0), (0, 0), (0, 0)))
    two = jnp.eye(2, dtype=BF16)
    up = jnp.einsum(
        "uldcrp,vw,mn->drcvmpwunl", ks8.reshape(legs, PACK, pairs, 2, legs, phys), two, two
    ).reshape(pairs * legs * 8 * phys, 2 * legs * 2 * PACK)
    kd = jnp.pad(ks, ((0, 0), (0, 0), (0, PACK - legs), (0, 0), (0, 0)))
    down = jnp.einsum("vwmnesp,dc->sdevmcwnp", kd.reshape(pairs, 2, pairs, 2, PACK, legs, phys), two).reshape(
        legs * 2 * PACK, pairs * pairs * 8 * phys
    )

    block = 8
    wide = block * LANES
    whole = lambda a: pl.BlockSpec(a.shape, lambda i: (0,) * a.ndim)
    image, squares = pl.pallas_call(
        functools.partial(chain, legs, block),
        grid=(half // block,),
        in_specs=[
            pl.BlockSpec((block * rows, chi), lambda i: (i, 0)),
            whole(ms),
            whole(up),
            whole(down),
            whole(rp),
        ],
        out_specs=[
            pl.BlockSpec((block * rows, chi), lambda i: (i, 0)),
            pl.BlockSpec((8, chi), lambda i: (0, 0)),
        ],
        out_shape=[
            jax.ShapeDtypeStruct((half * rows, chi), F32),
            jax.ShapeDtypeStruct((8, chi), F32),
        ],
        scratch_shapes=[
            pltpu.VMEM((chi, legs * legs * LANES), BF16),
            pltpu.VMEM((pairs, pairs, 2 * legs, 2 * PACK, wide), BF16),
            pltpu.VMEM((pairs * legs, pairs * pairs, 8 * phys, wide), BF16),
            pltpu.VMEM((block * rows, legs * legs * LANES), BF16),
        ],
        compiler_params=pltpu.CompilerParams(
            dimension_semantics=("arbitrary",), vmem_limit_bytes=56 * 1024 * 1024
        ),
    )(lp, ms, up, down, rp)

    sums = lax.all_gather(jnp.sum(squares).reshape(1), ("col", "sec"), axis=0, tiled=True)
    columns = lax.axis_size("col")
    meansq = jnp.sum(sums.reshape(columns, -1), axis=1) / (chi * legs * legs * chi)
    log_norm = jnp.mean(0.5 * jnp.log(meansq + 1e-06))
    mine = lax.dynamic_slice_in_dim(meansq, lax.axis_index("col"), 1, 0)[0]
    scale = lax.rsqrt(mine + 1e-06)
    image = image.reshape(half, legs, PACK, chi)[:, :, :legs, :]
    new_mps = (image * scale).astype(BF16)[None]
    return (new_mps, log_norm)


def solution(mesh):
    placed = (
        P("col", "sec", None, None, None),
        P("col", None, None, None, None, None),
        P("col", "sec", None, None, None),
        P("col", None, None, None, "sec"),
        P("col", None),
        P("col", None),
        P("col", None),
        P("col", None, None),
    )
    return jax.shard_map(
        local,
        mesh=mesh,
        in_specs=placed,
        out_specs=(P("col", "sec", None, None, None), P()),
        check_vma=False,
    )
```

time: 157 us -> 119 us (0.76)
  matrix products: 89.7 us -> 0 us
  Pallas kernels: 0 us -> 38.7 us
  local copies, waits for them, and re-layouts: 1.48 us -> 11.7 us
  other arithmetic: 4.45 us -> 12.3 us
  blocking collectives: 48.6 us -> 45.2 us
  starting transfers between devices: 9.52 us -> 7.55 us
    dot_general x4 -> x0, matrix products: 89.7 us -> none  [the longest x1 38.6 us: absorb(): jnp.einsum('xmvbdrp,vmesp->xbdres', second, masked_ket, preferred_element...]
    psum x2 -> x0, blocking collectives: 43.2 us -> none  [the longest x1 40.1 us: local(): total = lax.psum(jnp.sum(logs), 'col')]
    unnamed x0 -> x1, blocking collectives: none -> 39.8 us
    pallas_call x0 -> x1, Pallas kernels: none -> 38.7 us  [local(): pl.pallas_call(functools.partial(chain, legs, block), grid=(half // block...]
    reshape x0 -> x6, local copies, waits for them, and re-layouts: none -> 4.15 us  [the longest x1 1.79 us: local(): up = jnp.einsum('uldcrp,vw,mn->drcvmpwunl', ks8.reshape(legs, PACK, pairs...]
    pad x0 -> x5, local copies, waits for them, and re-layouts: none -> 3.69 us  [the longest x1 1.36 us: local(): jnp.pad(rp, ((0, 0), (0, 0), (0, LANES - chi), (0, 0)))]
    broadcast_in_dim x0 -> x1, other arithmetic: none -> 2.32 us  [local(): new_mps = (image * scale).astype(BF16)[None]]
    reduce_sum x0 -> x3, other arithmetic: none -> 2.02 us  [the longest x1 1.28 us: local(): jnp.sum(squares).reshape(1)]
  transfers between devices with their start and end apart: 4 -> 2, of which waited for: 0 -> 0; matrix products, arithmetic and copies ran while one was open for 49% -> 12% of each run, Pallas kernels for 0% -> 0%
where the time goes in v1:
time: 119 us
  blocking collectives  45.2 us (38%)
  Pallas kernels  38.7 us (33%)
  other arithmetic  12.3 us (10%)
  local copies, waits for them, and re-layouts  11.7 us (10%)
  starting transfers between devices  7.55 us (6%)
  between operations  3.21 us (3%)
    unnamed x1, blocking collectives  39.8 us
    pallas_call x1, Pallas kernels, local(): pl.pallas_call(functools.partial(chain, legs, block), grid=(half // block...  38.7 us
    ppermute x2, starting transfers between devices, from_behind(): return lax.ppermute(x, axis, [(i, (i + by) % count) for i in range(count)])  7.55 us
    all_gather x1, blocking collectives, local(): full_mps = lax.all_gather(mps, 'sec', axis=1, tiled=True)[0]  2.78 us
    all_gather x1, blocking collectives, local(): right = lax.all_gather(arrived, 'sec', axis=4, tiled=True)[0]  2.64 us
  transfers between devices with their start and end apart: 2, of which 0 were waited for; matrix products, arithmetic and copies ran while one was open for 12% of the time, Pallas kernels for 0%

profile of v1, /device:TPU:0, one launch (start us, length us, event | category | flops | bytes accessed | tf_op | source)
XLA Modules:
  0.0 118.6 jit_solution(17705347570053464299)
XLA Ops:
  0.6 7.0 %collective-permute-start.1 = (bf16[1,96,6,6,48]{1,4,3,2,0:T(8,128)(2,1)}, bf16[1,96,6,6,48]{1,4,3,2,0:T(8,128)(2,1)}, u32[]{:S(2)}, u32[]{:S(2)}) collective-permute-start(bf16[1,96,6,6,48]{1,4,3,2,0:T(8,128)(2,1)} %param.11), channel_id=1, source_target_pairs={{0,30},{2,0},{4,2},{6,4},{8,6},{10,8},{12,10},{14,12},{16,14},{18,... | collective-permute-start | bytes 995336 | tf_op jit(solution)/shard_map/ppermute | solution.py:18
  7.6 0.8 pad_add_fusion
  8.4 0.5 collective-permute-start
  8.9 0.8 slice_bitcast_fusion.3
  9.7 0.7 broadcast_add_fusion.2
  10.4 0.7 broadcast_add_fusion.3
  11.2 0.7 broadcast_subtract_fusion.2
  11.9 0.7 dynamic-slice_bitcast_fusion
  12.6 0.1 broadcast_subtract_fusion.1
  12.7 0.1 copy.36
  12.8 0.1 broadcast_multiply_fusion
  12.9 1.2 compare_select_fusion.2
  14.1 0.0 copy-start
  14.1 2.8 %all_gather.9 = bf16[1,96,6,6,96]{4,1,3,2,0:T(8,128)(2,1)S(1)} all-gather(bf16[1,48,6,6,96]{4,1,3,2,0:T(8,128)(2,1)} %param.8), channel_id=1, replica_groups=mesh['col'=16,'sec'=2] {'sec'}, dimensions={1}, use_global_device_ids=true | all-gather | bytes 995328 | tf_op jit(solution)/shard_map/all_gather | solution.py:73
  16.9 0.2 copy.44
  17.1 1.0 pad.20.clone
  18.0 0.0 collective-permute-done
  18.0 0.1 slice_bitcast_fusion.1
  18.1 0.1 broadcast_add_fusion.1
  18.2 0.0 copy-done
  18.2 0.2 compare_select_fusion.3
  18.4 0.1 pad.22
  18.6 0.1 pad.23
  18.7 0.8 copy.38
  19.6 0.5 copy.39
  20.1 0.4 multiply_bitcast_fusion.1
  20.5 1.3 %multiply_bitcast_fusion = bf16[3,6,2,2,2,2,2,6,2,8]{9,8,7,6,5,4,3,2,1,0:T(2,128)(2,1)S(1)} fusion(bf16[6,8,3,2,6,2]{1,0,5,3,4,2:T(8,128)(2,1)S(1)} %copy.38, bf16[2,2,2,2]{1,3,0,2:T(2,128)(2,1)S(1)} %broadcast_multiply_fusion), kind=kLoop, calls=%fused_computation | loop fusion | flops 55296 | bytes 117536 | tf_op jit(solution)/shard_map/uldcrp,vw,mn->drcvmpwunl/transpose | solution.py:117
  21.9 0.1 slice_bitcast_fusion
  21.9 0.1 broadcast_add_fusion
  22.0 1.8 %reshape.267.up_ref = bf16[288,192]{1,0:T(8,128)(2,1)} reshape(bf16[3,6,2,2,2,2,2,6,2,8]{9,8,7,6,5,4,3,2,1,0:T(2,128)(2,1)S(1)} %multiply_bitcast_fusion) | data formatting | bytes 221184 | tf_op jit(solution)/shard_map/reshape | solution.py:119
  23.8 0.2 reshape.269
  24.0 0.7 copy.41.down_ref
  24.8 0.1 broadcast_subtract_fusion
  24.8 0.0 collective-permute-done.1
  24.8 2.6 %all_gather.10 = bf16[1,96,6,6,96]{1,4,3,2,0:T(8,128)(2,1)S(1)} all-gather(bf16[1,96,6,6,48]{1,4,3,2,0:T(8,128)(2,1)} %collective-permute-done.1), channel_id=1, replica_groups=mesh['col'=16,'sec'=2] {'sec'}, dimensions={4}, use_global_device_ids=true | all-gather | bytes 995328 | tf_op jit(solution)/shard_map/all_gather | solution.py:82
  27.5 0.6 copy.40
  28.1 1.4 %compare_select_fusion = (bf16[6,6,96,96]{3,2,1,0:T(8,128)(2,1)S(1)}, bf16[6,6,96,96]{3,2,1,0:T(8,128)(2,1)S(1)}) fusion(bf16[1,96,6,6,96]{4,1,3,2,0:T(8,128)(2,1)S(1)} %copy.40, s32[96]{0:T(128)S(1)} %get-tuple-element.6, s32[6,6,96]{2,1,0:T(8,128)S(1)} %broadcast_subtract_fusion, bf16[1,96,6,6,96]{4,1,3,2,0:T(8,128)(2,1)S(1)} %all_gather.9, ...), kind=kLoop, calls=%fused_computation.1 | loop fusion | flops 1327104 | bytes 2682624 | tf_op jit(solution)/shard_map/jit(_where)/select_n | solution.py:107
  29.4 1.1 pad.21.mps_ref
  30.5 1.4 %pad.24 = bf16[6,6,128,96]{3,2,1,0:T(8,128)(2,1)} pad(bf16[6,6,96,96]{3,2,1,0:T(8,128)(2,1)S(1)} %get-tuple-element.14, bf16[]{:T(256)} %constant.12.clone.1), padding=0_0x0_0x0_32x0_0 | pad | bytes 1548290 | tf_op jit(solution)/shard_map/jit(_pad)/pad | solution.py:108
  31.9 38.7 %shard_map.98 = (f32[2304,96]{1,0:T(8,128)}, f32[8,96]{1,0:T(8,128)}) custom-call(bf16[2304,96]{1,0:T(8,128)(2,1)} %bitcast.47, bf16[36,96,128]{2,1,0:T(8,128)(2,1)} %pad.21.mps_ref, bf16[288,192]{1,0:T(8,128)(2,1)} %reshape.267.up_ref, bf16[96,144]{1,0:T(8,128)(2,1)} %copy.41.down_ref, bf16[4608,96]{1,0:T(8,128)(2,1)} %bitcast.45), custom_call_target="tpu_custom_call" | custom-call | tf_op jit(solution)/shard_map/pallas_call | solution.py:128
  70.6 1.3 %reduce_sum.27 = f32[]{:T(128)} reduce(f32[8,96]{1,0:T(8,128)} %get-tuple-element.5, f32[]{:T(128)} %constant.26.clone.1), dimensions={0,1}, to_apply=%region_0.1 | reduce | flops 767 | bytes 3080 | tf_op jit(solution)/shard_map/reduce_sum | solution.py:157
  71.9 0.8 dynamic-update-slice
  72.6 39.8 %all-reduce.5 = f32[32]{0:T(128)S(1)} all-reduce(f32[32]{0:T(128)S(1)} %dynamic-update-slice), channel_id=1, replica_groups=mesh['col'=16,'sec'=2] {'col','sec'}, use_global_device_ids=true, to_apply=%add.5 | all-reduce | flops 32 | bytes 256
  112.4 0.1 reshape.273
  112.5 0.1 reduce_sum.28
  112.6 0.6 multiply_reduce_fusion
  113.3 0.6 dynamic_slice.7
  114.5 2.3 %fusion.1 = bf16[1,48,6,6,96]{4,1,3,2,0:T(8,128)(2,1)} fusion(f32[48,6,6,96]{3,2,1,0:T(8,128)} %bitcast.48, f32[]{:T(128)} %bitcast.24), kind=kLoop, calls=%fused_computation.6 | loop fusion | flops 331776 | bytes 995332 | tf_op jit(solution)/shard_map/broadcast_in_dim | solution.py:164
  (3 shorter events, 0.0 us)
Async XLA Ops:
  0.6 24.2 %collective-permute-start.1 = (bf16[1,96,6,6,48]{1,4,3,2,0:T(8,128)(2,1)}, bf16[1,96,6,6,48]{1,4,3,2,0:T(8,128)(2,1)}, u32[]{:S(2)}, u32[]{:S(2)}) collective-permute-start(bf16[1,96,6,6,48]{1,4,3,2,0:T(8,128)(2,1)} %param.11), channel_id=1, source_target_pairs={{0,30},{2,0},{4,2},{6,4},{8,6},{10,8},{12,10},{14,12},{16,14},{18,... | collective-permute-start | bytes 995336 | tf_op jit(solution)/shard_map/ppermute | solution.py:18
  8.4 9.6 %collective-permute-start = (s32[1,198]{1,0:T(1,128)S(1)}, s32[1,198]{1,0:T(1,128)S(1)}, u32[]{:S(2)}, u32[]{:S(2)}) collective-permute-start(s32[1,198]{1,0:T(1,128)S(1)} %pad_add_fusion), channel_id=1, source_target_pairs={{0,30},{2,0},{4,2},{6,4},{8,6},{10,8},{12,10},{14,12},{16,14},{18,... | collective-permute-start | bytes 2384 | tf_op jit(solution)/shard_map/ppermute | solution.py:18
  14.1 4.1 %copy-start = (bf16[1,6,6,6,6,2]{4,5,3,2,1,0:T(2,128)(2,1)S(1)}, bf16[1,6,6,6,6,2]{4,5,3,2,1,0:T(2,128)(2,1)}, u32[]{:S(2)}) copy-start(bf16[1,6,6,6,6,2]{4,5,3,2,1,0:T(2,128)(2,1)} %param.9) | copy-start | bytes 15556

commit v2 on v1

--- a/solution.py
+++ b/solution.py
@@ -18,7 +18,28 @@
     return lax.ppermute(x, axis, [(i, (i + by) % count) for i in range(count)])
 
 
-def chain(legs, block, left_ref, mps_ref, up_ref, down_ref, right_ref, out_ref, sq_ref, mps_s, w1, w2, w3):
+def chain(
+    legs, block, count, cols, secs, left_ref, mps_ref, up_ref, down_ref, right_ref, out_ref, log_ref,
+    mps_s, w1, w2, w3, image_s, sq_ref, stage, slots, send_sem, recv_sem,
+):
+    total = cols * secs
+    me_col, me_sec = lax.axis_index("col"), lax.axis_index("sec")
+    me = me_col * secs + me_sec
+    barrier = pltpu.get_barrier_semaphore()
+    step = pl.program_id(0)
+
+    def other(k):
+        at = lax.rem(me + k, total)
+        return at, (at // secs, lax.rem(at, secs))
+
+    @pl.when(step == 0)
+    def _():
+        def greet(k, _):
+            pl.semaphore_signal(barrier, inc=1, device_id=other(k)[1], device_id_type=pl.DeviceIdType.MESH)
+            return 0
+
+        lax.fori_loop(1, total, greet, 0)
+
     pairs = legs // 2
     rows = legs * PACK
     wide = block * LANES
@@ -64,8 +85,62 @@
                     ]
 
     image = jnp.dot(w3[...], right_ref[...], preferred_element_type=F32)
-    out_ref[...] = image
-    sq_ref[...] += jnp.sum((image * image).reshape(block * rows // 8, 8, image.shape[1]), axis=0)
+    here = block * rows
+    image_s[pl.ds(pl.multiple_of(step * here, here), here), :] = image
+    sq_ref[...] += jnp.sum((image * image).reshape(here // 8, 8, image.shape[1]), axis=0)
+
+    @pl.when(step == pl.num_programs(0) - 1)
+    def _():
+        mine = jnp.sum(jnp.sum(sq_ref[...], axis=0, keepdims=True), axis=1, keepdims=True)
+        stage[...] = jnp.broadcast_to(mine, stage.shape)
+        slots[me] = jnp.broadcast_to(mine, stage.shape)
+        pl.semaphore_wait(barrier, total - 1)
+
+        def copy_to(k):
+            at, where = other(k)
+            return pltpu.make_async_remote_copy(
+                src_ref=stage,
+                dst_ref=slots.at[me],
+                send_sem=send_sem.at[k],
+                recv_sem=recv_sem.at[me],
+                device_id=where,
+                device_id_type=pl.DeviceIdType.MESH,
+            )
+
+        def send(k, _):
+            copy_to(k).start()
+            return 0
+
+        def receive(k, _):
+            at, where = other(k)
+            pltpu.make_async_remote_copy(
+                src_ref=stage,
+                dst_ref=slots.at[at],
+                send_sem=send_sem.at[k],
+                recv_sem=recv_sem.at[at],
+                device_id=where,
+                device_id_type=pl.DeviceIdType.MESH,
+            ).wait_recv()
+            return 0
+
+        def sent(k, _):
+            copy_to(k).wait_send()
+            return 0
+
+        lax.fori_loop(1, total, send, 0)
+        lax.fori_loop(1, total, receive, 0)
+        lax.fori_loop(1, total, sent, 0)
+        site = slots[me_col * secs]
+        for k in range(1, secs):
+            site = site + slots[me_col * secs + k]
+        scale = lax.rsqrt(site[0:1, 0:1] / count + 1e-06)
+        sums = jnp.sum(slots[...].reshape(cols, secs, 8, LANES), axis=1) / count
+        log_ref[...] = jnp.sum(0.5 * jnp.log(sums + 1e-06), axis=0) / cols
+        half = image_s.shape[0] // rows
+        for d in range(legs):
+            for e in range(legs):
+                values = image_s[pl.ds(d * PACK + e, half, stride=rows), :]
+                out_ref[d * legs + e] = (values * scale).astype(BF16)
 
 
 def local(mps, ket, left_proj, right_proj, bond_charge, new_charge, link_charge, vert_charge):
@@ -124,9 +199,14 @@
 
     block = 8
     wide = block * LANES
-    whole = lambda a: pl.BlockSpec(a.shape, lambda i: (0,) * a.ndim)
-    image, squares = pl.pallas_call(
-        functools.partial(chain, legs, block),
+    cols, secs = lax.axis_size("col"), lax.axis_size("sec")
+    whole = lambda a: pl.BlockSpec(a.shape, lambda i: (0,) * len(a.shape))
+    outs = [
+        jax.ShapeDtypeStruct((legs * legs, half, chi), BF16),
+        jax.ShapeDtypeStruct((8, LANES), F32),
+    ]
+    image, logs = pl.pallas_call(
+        functools.partial(chain, legs, block, chi * legs * legs * chi, cols, secs),
         grid=(half // block,),
         in_specs=[
             pl.BlockSpec((block * rows, chi), lambda i: (i, 0)),
@@ -135,34 +215,29 @@
             whole(down),
             whole(rp),
         ],
-        out_specs=[
-            pl.BlockSpec((block * rows, chi), lambda i: (i, 0)),
-            pl.BlockSpec((8, chi), lambda i: (0, 0)),
-        ],
-        out_shape=[
-            jax.ShapeDtypeStruct((half * rows, chi), F32),
-            jax.ShapeDtypeStruct((8, chi), F32),
-        ],
+        out_specs=[whole(outs[0]), whole(outs[1])],
+        out_shape=outs,
         scratch_shapes=[
             pltpu.VMEM((chi, legs * legs * LANES), BF16),
             pltpu.VMEM((pairs, pairs, 2 * legs, 2 * PACK, wide), BF16),
             pltpu.VMEM((pairs * legs, pairs * pairs, 8 * phys, wide), BF16),
             pltpu.VMEM((block * rows, legs * legs * LANES), BF16),
+            pltpu.VMEM((half * rows, chi), F32),
+            pltpu.VMEM((8, chi), F32),
+            pltpu.VMEM((8, LANES), F32),
+            pltpu.VMEM((cols * secs, 8, LANES), F32),
+            pltpu.SemaphoreType.DMA((cols * secs,)),
+            pltpu.SemaphoreType.DMA((cols * secs,)),
         ],
         compiler_params=pltpu.CompilerParams(
-            dimension_semantics=("arbitrary",), vmem_limit_bytes=56 * 1024 * 1024
+            dimension_semantics=("arbitrary",),
+            vmem_limit_bytes=56 * 1024 * 1024,
+            collective_id=0,
+            has_side_effects=True,
         ),
     )(lp, ms, up, down, rp)
-
-    sums = lax.all_gather(jnp.sum(squares).reshape(1), ("col", "sec"), axis=0, tiled=True)
-    columns = lax.axis_size("col")
-    meansq = jnp.sum(sums.reshape(columns, -1), axis=1) / (chi * legs * legs * chi)
-    log_norm = jnp.mean(0.5 * jnp.log(meansq + 1e-06))
-    mine = lax.dynamic_slice_in_dim(meansq, lax.axis_index("col"), 1, 0)[0]
-    scale = lax.rsqrt(mine + 1e-06)
-    image = image.reshape(half, legs, PACK, chi)[:, :, :legs, :]
-    new_mps = (image * scale).astype(BF16)[None]
-    return (new_mps, log_norm)
+    new_mps = image.reshape(legs, legs, half, chi).transpose(2, 0, 1, 3)[None]
+    return (new_mps, logs[0, 0])
 
 
 def solution(mesh):

time: 119 us -> 82.7 us (0.69)
  blocking collectives: 45.2 us -> 5.42 us
  Pallas kernels: 38.7 us -> 47.4 us
  other arithmetic: 12.3 us -> 7.92 us
  between operations: 3.21 us -> 0.73 us
  local copies, waits for them, and re-layouts: 11.7 us -> 13.3 us
    unnamed x1 -> x0, blocking collectives: 39.8 us -> none
    pallas_call x1, Pallas kernels: 38.7 us -> 47.4 us  [local(): pl.pallas_call(functools.partial(chain, legs, block, chi * legs * legs *...]
    broadcast_in_dim x1 -> x0, other arithmetic: 2.32 us -> none  [local(): new_mps = (image * scale).astype(BF16)[None]]
    reduce_sum x3 -> x0, other arithmetic: 2.02 us -> none  [the longest x1 1.28 us: local(): jnp.sum(squares).reshape(1)]
  transfers between devices with their start and end apart: 2 -> 2, of which waited for: 0 -> 0; matrix products, arithmetic and copies ran while one was open for 12% -> 17% of each run, Pallas kernels for 0% -> 0%
where the time goes in v2:
time: 82.7 us; the launch traced here: 82.3 us
  Pallas kernels  47.4 us (57%)
  local copies, waits for them, and re-layouts  13.3 us (16%)
  other arithmetic  7.92 us (10%)
  starting transfers between devices  7.55 us (9%)
  blocking collectives  5.42 us (7%)
    pallas_call x1, Pallas kernels, local(): pl.pallas_call(functools.partial(chain, legs, block, chi * legs * legs *...  47.4 us
    ppermute x2, starting transfers between devices, from_behind(): return lax.ppermute(x, axis, [(i, (i + by) % count) for i in range(count)])  7.55 us
    all_gather x1, blocking collectives, local(): full_mps = lax.all_gather(mps, 'sec', axis=1, tiled=True)[0]  2.78 us
    all_gather x1, blocking collectives, local(): right = lax.all_gather(arrived, 'sec', axis=4, tiled=True)[0]  2.64 us
    unnamed x4, local copies, waits for them, and re-layouts  2 us
    reshape x1, local copies, waits for them, and re-layouts, local(): up = jnp.einsum('uldcrp,vw,mn->drcvmpwunl', ks8.reshape(legs, PACK, pairs...  1.79 us
  transfers between devices with their start and end apart: 2, of which 0 were waited for; matrix products, arithmetic and copies ran while one was open for 17% of the time, Pallas kernels for 0%

profile of v2, /device:TPU:0, one launch (start us, length us, event | category | flops | bytes accessed | tf_op | source)
XLA Modules:
  0.0 82.3 jit_solution(8831552096718655681)
XLA Ops:
  0.6 7.0 %collective-permute-start.1 = (bf16[1,96,6,6,48]{1,4,3,2,0:T(8,128)(2,1)}, bf16[1,96,6,6,48]{1,4,3,2,0:T(8,128)(2,1)}, u32[]{:S(2)}, u32[]{:S(2)}) collective-permute-start(bf16[1,96,6,6,48]{1,4,3,2,0:T(8,128)(2,1)} %param.11), channel_id=1, source_target_pairs={{0,30},{2,0},{4,2},{6,4},{8,6},{10,8},{12,10},{14,12},{16,14},{18,... | collective-permute-start | bytes 995336 | tf_op jit(solution)/shard_map/ppermute | solution.py:18
  7.6 0.8 pad_add_fusion
  8.4 0.5 collective-permute-start
  8.9 0.8 slice_bitcast_fusion.3
  9.7 0.7 broadcast_add_fusion.2
  10.4 0.7 broadcast_add_fusion.3
  11.2 0.7 broadcast_subtract_fusion.2
  11.9 0.7 dynamic-slice_bitcast_fusion
  12.6 0.1 broadcast_subtract_fusion.1
  12.7 0.1 copy.33
  12.8 0.1 broadcast_multiply_fusion
  12.9 1.2 %compare_select_fusion.2 = bf16[48,6,6,96]{3,0,1,2:T(8,128)(2,1)S(1)} fusion(bf16[1,48,96,6,6]{2,1,4,3,0:T(8,128)(2,1)} %param.10, s32[6,6,96]{2,0,1:T(8,128)S(1)} %broadcast_subtract_fusion.2, s32[48]{0:T(128)S(1)} %dynamic-slice_bitcast_fusion), kind=kLoop, calls=%fused_computation.3 | loop fusion | flops 331776 | bytes 677568 | tf_op jit(solution)/shard_map/jit(_where)/select_n | solution.py:176
  14.1 0.0 copy-start
  14.1 2.8 %all_gather.6 = bf16[1,96,6,6,96]{4,1,3,2,0:T(8,128)(2,1)S(1)} all-gather(bf16[1,48,6,6,96]{4,1,3,2,0:T(8,128)(2,1)} %param.8), channel_id=1, replica_groups=mesh['col'=16,'sec'=2] {'sec'}, dimensions={1}, use_global_device_ids=true | all-gather | bytes 995328 | tf_op jit(solution)/shard_map/all_gather | solution.py:148
  16.9 0.2 copy.39
  17.1 1.0 %pad.20.clone = bf16[48,6,8,96]{3,2,1,0:T(8,128)(2,1)} pad(bf16[48,6,6,96]{3,2,1,0:T(8,128)(2,1)S(1)} %copy.39, bf16[]{:T(256)} %constant.12.clone.1), padding=0_0x0_0x0_2x0_0 | pad | bytes 774146 | tf_op jit(solution)/shard_map/jit(_pad)/pad | solution.py:177
  18.0 0.0 collective-permute-done
  18.0 0.1 slice_bitcast_fusion.1
  18.1 0.1 broadcast_add_fusion.1
  18.2 0.0 copy-done
  18.2 0.2 compare_select_fusion.3
  18.4 0.1 pad.22
  18.6 0.1 pad.23
  18.7 0.8 %copy.35 = bf16[6,8,3,2,6,2]{1,0,5,3,4,2:T(8,128)(2,1)S(1)} copy(bf16[6,8,3,2,6,2]{4,5,3,2,1,0:T(2,128)(2,1)S(1)} %bitcast.49) | data formatting | bytes 13824 | tf_op jit(solution)/shard_map/reshape | solution.py:193
  19.6 0.5 copy.36
  20.1 0.4 multiply_bitcast_fusion.1
  20.5 1.3 %multiply_bitcast_fusion = bf16[3,6,2,2,2,2,2,6,2,8]{9,8,7,6,5,4,3,2,1,0:T(2,128)(2,1)S(1)} fusion(bf16[6,8,3,2,6,2]{1,0,5,3,4,2:T(8,128)(2,1)S(1)} %copy.35, bf16[2,2,2,2]{1,3,0,2:T(2,128)(2,1)S(1)} %broadcast_multiply_fusion), kind=kLoop, calls=%fused_computation | loop fusion | flops 55296 | bytes 117536 | tf_op jit(solution)/shard_map/uldcrp,vw,mn->drcvmpwunl/transpose | solution.py:192
  21.9 0.1 slice_bitcast_fusion
  21.9 0.1 broadcast_add_fusion
  22.0 1.8 %reshape.258.up_ref = bf16[288,192]{1,0:T(8,128)(2,1)} reshape(bf16[3,6,2,2,2,2,2,6,2,8]{9,8,7,6,5,4,3,2,1,0:T(2,128)(2,1)S(1)} %multiply_bitcast_fusion) | data formatting | bytes 221184 | tf_op jit(solution)/shard_map/reshape | solution.py:194
  23.8 0.2 reshape.260
  24.0 0.7 copy.38.down_ref
  24.8 0.1 broadcast_subtract_fusion
  24.8 0.0 collective-permute-done.1
  24.8 2.6 %all_gather.7 = bf16[1,96,6,6,96]{1,4,3,2,0:T(8,128)(2,1)S(1)} all-gather(bf16[1,96,6,6,48]{1,4,3,2,0:T(8,128)(2,1)} %collective-permute-done.1), channel_id=1, replica_groups=mesh['col'=16,'sec'=2] {'sec'}, dimensions={4}, use_global_device_ids=true | all-gather | bytes 995328 | tf_op jit(solution)/shard_map/all_gather | solution.py:157
  27.5 0.6 copy.37
  28.1 1.4 %compare_select_fusion = (bf16[6,6,96,96]{3,2,1,0:T(8,128)(2,1)S(1)}, bf16[6,6,96,96]{3,2,1,0:T(8,128)(2,1)S(1)}) fusion(bf16[1,96,6,6,96]{4,1,3,2,0:T(8,128)(2,1)S(1)} %copy.37, s32[96]{0:T(128)S(1)} %get-tuple-element.6, s32[6,6,96]{2,1,0:T(8,128)S(1)} %broadcast_subtract_fusion, bf16[1,96,6,6,96]{4,1,3,2,0:T(8,128)(2,1)S(1)} %all_gather.6, ...), kind=kLoop, calls=%fused_computation.1 | loop fusion | flops 1327104 | bytes 2682624 | tf_op jit(solution)/shard_map/jit(_where)/select_n | solution.py:182
  29.4 1.1 %pad.21.mps_ref = bf16[36,96,128]{2,1,0:T(8,128)(2,1)} pad(bf16[36,96,96]{2,1,0:T(8,128)(2,1)S(1)} %bitcast.46, bf16[]{:T(256)} %constant.12.clone.1), padding=0_0x0_0x0_32 | pad | bytes 1548290 | tf_op jit(solution)/shard_map/jit(_pad)/pad | solution.py:171
  30.6 1.3 %pad.24 = bf16[6,6,128,96]{3,2,1,0:T(8,128)(2,1)} pad(bf16[6,6,96,96]{3,2,1,0:T(8,128)(2,1)S(1)} %get-tuple-element.12, bf16[]{:T(256)} %constant.12.clone.1), padding=0_0x0_0x0_32x0_0 | pad | bytes 1548290 | tf_op jit(solution)/shard_map/jit(_pad)/pad | solution.py:183
  31.9 47.4 %shard_map.98 = (bf16[36,48,96]{2,1,0:T(8,128)(2,1)}, f32[8,128]{1,0:T(8,128)}) custom-call(bf16[2304,96]{1,0:T(8,128)(2,1)} %bitcast.47, bf16[36,96,128]{2,1,0:T(8,128)(2,1)} %pad.21.mps_ref, bf16[288,192]{1,0:T(8,128)(2,1)} %reshape.258.up_ref, bf16[96,144]{1,0:T(8,128)(2,1)} %copy.38.down_ref, bf16[4608,96]{1,0:T(8,128)(2,1)} %bitcast.45), custom_call_target="tpu_custom_call" | custom-call | tf_op jit(solution)/shard_map/pallas_call | solution.py:208
  79.3 1.2 %slice.26 = f32[1,1]{1,0:T(1,128)} slice(f32[8,128]{1,0:T(8,128)} %get-tuple-element.5), slice={[0:1], [0:1]} | slice | bytes 8 | tf_op jit(solution)/shard_map/slice | solution.py:240
  80.5 1.8 %copy.41 = bf16[1,48,6,6,96]{4,1,3,2,0:T(8,128)(2,1)} copy(bf16[1,48,6,6,96]{4,1,3,2,0:T(8,128)(2,1)} %bitcast.50) | data formatting | bytes 663552
  (2 shorter events, 0.0 us)
Async XLA Ops:
  0.6 24.2 %collective-permute-start.1 = (bf16[1,96,6,6,48]{1,4,3,2,0:T(8,128)(2,1)}, bf16[1,96,6,6,48]{1,4,3,2,0:T(8,128)(2,1)}, u32[]{:S(2)}, u32[]{:S(2)}) collective-permute-start(bf16[1,96,6,6,48]{1,4,3,2,0:T(8,128)(2,1)} %param.11), channel_id=1, source_target_pairs={{0,30},{2,0},{4,2},{6,4},{8,6},{10,8},{12,10},{14,12},{16,14},{18,... | collective-permute-start | bytes 995336 | tf_op jit(solution)/shard_map/ppermute | solution.py:18
  8.4 9.6 %collective-permute-start = (s32[1,198]{1,0:T(1,128)S(1)}, s32[1,198]{1,0:T(1,128)S(1)}, u32[]{:S(2)}, u32[]{:S(2)}) collective-permute-start(s32[1,198]{1,0:T(1,128)S(1)} %pad_add_fusion), channel_id=1, source_target_pairs={{0,30},{2,0},{4,2},{6,4},{8,6},{10,8},{12,10},{14,12},{16,14},{18,... | collective-permute-start | bytes 2384 | tf_op jit(solution)/shard_map/ppermute | solution.py:18
  14.1 4.1 %copy-start = (bf16[1,6,6,6,6,2]{4,5,3,2,1,0:T(2,128)(2,1)S(1)}, bf16[1,6,6,6,6,2]{4,5,3,2,1,0:T(2,128)(2,1)}, u32[]{:S(2)}) copy-start(bf16[1,6,6,6,6,2]{4,5,3,2,1,0:T(2,128)(2,1)} %param.9) | copy-start | bytes 15556

commit v3 on v2

v3 whole, which is shorter than its diff:
```python
import functools

import jax
import jax.numpy as jnp
import numpy as np
from jax import lax
from jax.experimental import pallas as pl
from jax.experimental.pallas import tpu as pltpu
from jax.sharding import PartitionSpec as P

LANES = 128
PACK = 8
F32 = jnp.float32
BF16 = jnp.bfloat16


MESH = pl.DeviceIdType.MESH


def chain(
    legs, phys, block, count, cols, secs,
    left_ref, mps_ref, right_ref, ket_ref, bond_ref, fresh_ref, link_ref, link_sm, vert_sm,
    index_ref, pick2r, pick2c, same2, pick3r, pick3c, same3,
    out_ref, log_ref,
    left_s, mps_s, right_s, up_ref, down_ref, w1, w2, w3, image_s,
    charge_here, charge_next, mps_all, right_all, diff,
    stage, slots, near_send, near_recv, send_sem, recv_sem,
):
    total = cols * secs
    half, chi = left_ref.shape[1:]
    pairs = legs // 2
    rows = legs * PACK
    wide = block * LANES
    me_col, me_sec = lax.axis_index("col"), lax.axis_index("sec")
    me = me_col * secs + me_sec
    before = lax.rem(me_col + cols - 1, cols)
    barrier = pltpu.get_barrier_semaphore()
    step = pl.program_id(0)
    mine = pl.ds(pl.multiple_of(me_sec * half, 16), half)

    def other(k):
        at = lax.rem(me + k, total)
        return at, (at // secs, lax.rem(at, secs))

    def charge_copy():
        return pltpu.make_async_remote_copy(
            src_ref=charge_here, dst_ref=charge_next, send_sem=near_send.at[0], recv_sem=near_recv.at[0],
            device_id=(before, me_sec), device_id_type=MESH,
        )

    def mps_copy(k, source):
        return pltpu.make_async_remote_copy(
            src_ref=mps_ref, dst_ref=mps_all.at[source], send_sem=near_send.at[k],
            recv_sem=near_recv.at[1 + source],
            device_id=(me_col, lax.rem(me_sec + k, secs)), device_id_type=MESH,
        )

    def right_copy(t, source):
        return pltpu.make_async_remote_copy(
            src_ref=right_ref, dst_ref=right_all.at[source], send_sem=near_send.at[secs + t],
            recv_sem=near_recv.at[1 + secs + source],
            device_id=(before, t), device_id_type=MESH,
        )

    def down_rows(row):
        return jnp.broadcast_to(row, (LANES, LANES)).T

    @pl.when(step == 0)
    def _():
        def greet(k, _):
            pl.semaphore_signal(barrier, inc=1, device_id=other(k)[1], device_id_type=MESH)
            return 0

        lax.fori_loop(1, total, greet, 0)
        charge_here[...] = jnp.zeros_like(charge_here)
        charge_here[0:1, 0:chi] = bond_ref[...]
        charge_here[1:2, 0:chi] = fresh_ref[...]
        charge_here[2:3, 0:legs] = link_ref[...]
        here = charge_here[...].astype(F32)
        diff[...] = down_rows(here[1:2]) - here[0:1]
        left_s[...] = jnp.zeros_like(left_s)
        delta = diff[mine, 0:chi]
        for l in range(legs):
            for m in range(legs):
                gap = (link_sm[0, l] - link_sm[0, m]).astype(F32)
                value = jnp.where(delta == gap, left_ref[l * legs + m].astype(F32), 0.0)
                left_s[pl.ds(m * PACK + l, half, stride=rows), :] = value
        mps_s[...] = jnp.zeros_like(mps_s)
        pl.semaphore_wait(barrier, total - 1)
        charge_copy().start()
        for k in range(1, secs):
            mps_copy(k, me_sec).start()
        for t in range(secs):
            right_copy(t, me_sec).start()
        charge_copy().wait_recv()
        after = charge_next[...].astype(F32)
        diff[...] = after[0:1] - down_rows(here[0:1])

        def place(which, source):
            at = pl.ds(pl.multiple_of(which * half, 16), half)
            delta = diff[at, 0:chi]
            for u in range(legs):
                for v in range(legs):
                    gap = (vert_sm[0, u] - vert_sm[0, v]).astype(F32)
                    uv = u * legs + v
                    value = jnp.where(delta == gap, source[uv].astype(F32), 0.0)
                    mps_s[at, uv * LANES : uv * LANES + chi] = value.astype(BF16)

        place(me_sec, mps_ref)
        lower = index_ref[1].astype(F32)
        upper = jnp.zeros_like(lower)
        for i in range(legs):
            lower += jnp.where(index_ref[0] == i, vert_sm[1, i].astype(F32), 0.0)
            lower += jnp.where(index_ref[2] == i, after[2:3, i : i + 1], 0.0)
            upper += jnp.where(index_ref[3] == i, vert_sm[0, i].astype(F32), 0.0)
            upper += jnp.where(index_ref[4] == i, link_sm[0, i].astype(F32), 0.0)
        ket = jnp.where(upper == lower, ket_ref[...].astype(F32), 0.0).astype(BF16)
        grown = jnp.dot(pick2r[...], ket, preferred_element_type=F32).astype(BF16)
        up_ref[...] = (jnp.dot(grown, pick2c[...], preferred_element_type=F32) * same2[...]).astype(BF16)
        low = jnp.zeros(down_ref.shape, F32)
        for p in range(phys):
            grown = jnp.dot(pick3r[p], ket, preferred_element_type=F32).astype(BF16)
            low += jnp.dot(grown, pick3c[p], preferred_element_type=F32)
        down_ref[...] = (low * same3[...]).astype(BF16)
        for k in range(1, secs):
            source = lax.rem(me_sec + k, secs)
            mps_copy(k, source).wait_recv()
            place(source, mps_all.at[source])

    base = pl.multiple_of(step * (block * rows), block * rows)
    left = left_s[pl.ds(base, block * rows), :].astype(BF16)
    for u in range(legs):
        for vp in range(pairs):
            at = (u * legs + 2 * vp) * LANES
            part = jnp.dot(left, mps_s[:, at : at + 2 * LANES], preferred_element_type=F32).astype(BF16)
            for x in range(block):
                for mp in range(pairs):
                    lo = x * rows + mp * 2 * PACK
                    for v2 in range(2):
                        w1[vp, mp, v2 * legs + u, :, x * LANES : (x + 1) * LANES] = part[
                            lo : lo + 2 * PACK, v2 * LANES : (v2 + 1) * LANES
                        ]

    slab = w2.shape[2]

    def second(i, _):
        rhs = w1[i // pairs, i % pairs].reshape(2 * legs * 2 * PACK, wide)
        part = jnp.dot(up_ref[...], rhs, preferred_element_type=F32).astype(BF16)
        w2[:, i] = part.reshape(pairs * legs, slab, wide)
        return 0

    lax.fori_loop(0, pairs * pairs, second, 0)

    for dp in range(pairs):
        for r in range(legs):
            rhs = w2[dp * legs + r].reshape(pairs * pairs * slab, wide)
            part = jnp.dot(down_ref[...], rhs, preferred_element_type=F32).astype(BF16)
            for x in range(block):
                for s in range(legs):
                    lane = (r * legs + s) * LANES
                    row = pl.multiple_of(base + (x * rows + dp * 2 * PACK), 2 * PACK)
                    w3[pl.ds(row, 2 * PACK), lane : lane + LANES] = part[
                        s * 2 * PACK : (s + 1) * 2 * PACK, x * LANES : (x + 1) * LANES
                    ]

    @pl.when(step == pl.num_programs(0) - 1)
    def _():
        after = charge_next[...].astype(F32)
        diff[...] = down_rows(after[1:2]) - after[0:1]
        right_s[...] = jnp.zeros_like(right_s)
        for k in range(secs):
            right_copy(k, k).wait_recv()
            delta = diff[k * half : (k + 1) * half, 0:chi]
            for r in range(legs):
                for s in range(legs):
                    gap = after[2:3, r : r + 1] - after[2:3, s : s + 1]
                    rs = r * legs + s
                    value = jnp.where(delta == gap, right_all[k, rs].astype(F32), 0.0)
                    right_s[k * half : (k + 1) * half, rs * LANES : rs * LANES + chi] = value.astype(BF16)

        def last(i, square):
            at = pl.ds(pl.multiple_of(i * (block * rows), block * rows), block * rows)
            image = lax.dot_general(
                w3[at, :], right_s[...], (((1,), (1,)), ((), ())), preferred_element_type=F32
            )
            image_s[at, :] = image
            return square + jnp.sum((image * image).reshape(block * rows // 8, 8, chi), axis=0)

        square = lax.fori_loop(0, half // block, last, jnp.zeros((8, chi), F32))
        part = jnp.sum(jnp.sum(square, axis=0, keepdims=True), axis=1, keepdims=True)
        stage[...] = jnp.broadcast_to(part, stage.shape)
        slots[me] = jnp.broadcast_to(part, stage.shape)

        def copy_to(k):
            at, where = other(k)
            return pltpu.make_async_remote_copy(
                src_ref=stage,
                dst_ref=slots.at[me],
                send_sem=send_sem.at[k],
                recv_sem=recv_sem.at[me],
                device_id=where,
                device_id_type=pl.DeviceIdType.MESH,
            )

        def send(k, _):
            copy_to(k).start()
            return 0

        def receive(k, _):
            at, where = other(k)
            pltpu.make_async_remote_copy(
                src_ref=stage,
                dst_ref=slots.at[at],
                send_sem=send_sem.at[k],
                recv_sem=recv_sem.at[at],
                device_id=where,
                device_id_type=pl.DeviceIdType.MESH,
            ).wait_recv()
            return 0

        def sent(k, _):
            copy_to(k).wait_send()
            return 0

        lax.fori_loop(1, total, send, 0)
        lax.fori_loop(1, total, receive, 0)
        lax.fori_loop(1, total, sent, 0)
        charge_copy().wait_send()
        for k in range(1, secs):
            mps_copy(k, me_sec).wait_send()
        for t in range(secs):
            right_copy(t, me_sec).wait_send()
        site = slots[me_col * secs]
        for k in range(1, secs):
            site = site + slots[me_col * secs + k]
        scale = lax.rsqrt(site[0:1, 0:1] / count + 1e-06)
        sums = jnp.sum(slots[...].reshape(cols, secs, 8, LANES), axis=1) / count
        log_ref[...] = jnp.sum(0.5 * jnp.log(sums + 1e-06), axis=0) / cols
        for d in range(legs):
            for e in range(legs):
                values = image_s[pl.ds(d * PACK + e, half, stride=rows), :]
                out_ref[d * legs + e] = (values * scale).astype(BF16)


def picks(legs, phys):
    pairs = legs // 2
    eye = lambda n, m=None: np.eye(n, m, dtype=np.float32)
    d, p, r, u, l = np.meshgrid(*[np.arange(n) for n in (legs, phys, legs, legs, legs)], indexing="ij")
    shape = (legs * phys * legs, legs * legs)
    index = np.stack([d, p, r, u, l]).reshape((5,) + shape).astype(np.int32)
    two = np.ones(2, np.float32)
    dd = eye(legs).reshape(pairs, 2, legs)
    pick2r = np.einsum("icD,rR,v,m,pP->ircvmpDPR", dd, eye(legs), two, two, eye(phys)).reshape(-1, shape[0])
    pick2c = np.einsum("uU,lL,w,n->ulwUnL", eye(legs), eye(legs, PACK), two, two).reshape(shape[1], -1)
    same2 = np.einsum("i,c,p,vw,mn,u,l->icvmpwunl", np.ones(pairs * legs), two, np.ones(phys), eye(2), eye(2),
                      np.ones(legs), np.ones(PACK)).reshape(pick2r.shape[0], -1)
    pick3r = np.einsum("sR,c,De,qP->qsceDPR", eye(legs), two, eye(legs, PACK), eye(phys)).reshape(phys, -1, shape[0])
    pick3c = np.einsum("iav,jbm,c,qp->qvmijcabp", dd, dd, two, eye(phys)).reshape(phys, shape[1], -1)
    same3 = np.einsum("s,dc,e,i,a,p->sdeicap", np.ones(legs), eye(2), np.ones(PACK), np.ones(pairs * pairs),
                      np.ones(4), np.ones(phys)).reshape(pick3r.shape[1], -1)
    out = [jnp.asarray(index)]
    return out + [jnp.asarray(a, BF16) for a in (pick2r, pick2c, same2, pick3r, pick3c, same3)]


def local(mps, ket, left_proj, right_proj, bond_charge, new_charge, link_charge, vert_charge):
    half, chi, legs = left_proj.shape[1:4]
    phys = ket.shape[5]
    pairs = legs // 2
    rows = legs * PACK
    block = 8
    wide = block * LANES
    square = legs * legs
    cols, secs = lax.axis_size("col"), lax.axis_size("sec")
    arrays = [
        left_proj[0].transpose(2, 3, 0, 1).reshape(square, half, chi),
        mps[0].transpose(1, 2, 0, 3).reshape(square, half, chi),
        right_proj[0].transpose(1, 2, 3, 0).reshape(square, half, chi),
        ket[0].transpose(2, 4, 3, 0, 1).reshape(square * phys, square),
        bond_charge,
        new_charge,
        link_charge,
    ]
    small = [link_charge, vert_charge[0]]
    tables = picks(legs, phys)
    whole = lambda a: pl.BlockSpec(a.shape, lambda i: (0,) * len(a.shape))
    scalar = pl.BlockSpec(memory_space=pltpu.SMEM)
    outs = [jax.ShapeDtypeStruct((square, half, chi), BF16), jax.ShapeDtypeStruct((8, LANES), F32)]
    image, logs = pl.pallas_call(
        functools.partial(chain, legs, phys, block, chi * square * chi, cols, secs),
        grid=(half // block,),
        in_specs=[whole(a) for a in arrays] + [scalar] * 2 + [whole(a) for a in tables],
        out_specs=[whole(a) for a in outs],
        out_shape=outs,
        scratch_shapes=[
            pltpu.VMEM((half * rows, chi), F32),
            pltpu.VMEM((chi, square * LANES), BF16),
            pltpu.VMEM((chi, square * LANES), BF16),
            pltpu.VMEM(tables[3].shape, BF16),
            pltpu.VMEM(tables[6].shape, BF16),
            pltpu.VMEM((pairs, pairs, 2 * legs, 2 * PACK, wide), BF16),
            pltpu.VMEM((pairs * legs, pairs * pairs, 8 * phys, wide), BF16),
            pltpu.VMEM((half * rows, square * LANES), BF16),
            pltpu.VMEM((half * rows, chi), F32),
            pltpu.VMEM((8, LANES), jnp.int32),
            pltpu.VMEM((8, LANES), jnp.int32),
            pltpu.VMEM((secs, square, half, chi), BF16),
            pltpu.VMEM((secs, square, half, chi), BF16),
            pltpu.VMEM((LANES, LANES), F32),
            pltpu.VMEM((8, LANES), F32),
            pltpu.VMEM((cols * secs, 8, LANES), F32),
            pltpu.SemaphoreType.DMA((2 * secs,)),
            pltpu.SemaphoreType.DMA((1 + 2 * secs,)),
            pltpu.SemaphoreType.DMA((cols * secs,)),
            pltpu.SemaphoreType.DMA((cols * secs,)),
        ],
        compiler_params=pltpu.CompilerParams(
            dimension_semantics=("arbitrary",),
            vmem_limit_bytes=60 * 1024 * 1024,
            collective_id=0,
            has_side_effects=True,
        ),
    )(*arrays, *small, *tables)
    new_mps = image.reshape(legs, legs, half, chi).transpose(2, 0, 1, 3)[None]
    return (new_mps, logs[0, 0])


def solution(mesh):
    placed = (
        P("col", "sec", None, None, None),
        P("col", None, None, None, None, None),
        P("col", "sec", None, None, None),
        P("col", None, None, None, "sec"),
        P("col", None),
        P("col", None),
        P("col", None),
        P("col", None, None),
    )
    return jax.shard_map(
        local,
        mesh=mesh,
        in_specs=placed,
        out_specs=(P("col", "sec", None, None, None), P()),
        check_vma=False,
    )
```

time: 82.7 us -> 63.3 us (0.77)
  Pallas kernels: 47.4 us -> 57.7 us
  local copies, waits for them, and re-layouts: 13.3 us -> 4.74 us
  other arithmetic: 7.92 us -> 0 us
  starting transfers between devices: 7.55 us -> 0 us
  blocking collectives: 5.42 us -> 0 us
    pallas_call x1, Pallas kernels: 47.4 us -> 57.7 us  [local(): pl.pallas_call(functools.partial(chain, legs, phys, block, chi * square *...]
    ppermute x2 -> x0, starting transfers between devices: 7.55 us -> none  [from_behind(): return lax.ppermute(x, axis, [(i, (i + by) % count) for i in range(count)])]
    all_gather x2 -> x0, blocking collectives: 5.42 us -> none  [the longest x1 2.78 us: local(): full_mps = lax.all_gather(mps, 'sec', axis=1, tiled=True)[0]]
    pad x5 -> x0, local copies, waits for them, and re-layouts: 3.71 us -> none  [the longest x1 1.33 us: local(): jnp.pad(rp, ((0, 0), (0, 0), (0, LANES - chi), (0, 0)))]
    select_n x3 -> x0, other arithmetic: 2.8 us -> none  [the longest x1 1.38 us: local(): rp = jnp.where(keep, right.transpose(1, 2, 0, 3), 0)]
    reshape x5 -> x2, local copies, waits for them, and re-layouts: 4.07 us -> 1.75 us  [local(): ket[0].transpose(2, 4, 3, 0, 1).reshape(square * phys, square)]
    transpose x2 -> x0, other arithmetic: 1.79 us -> none  [the longest x1 1.35 us: local(): jnp.einsum('uldcrp,vw,mn->drcvmpwunl', ks8.reshape(legs, PACK, pairs, 2,...]
    add x5 -> x0, other arithmetic: 1.62 us -> none  [the longest x1 0.74 us: local(): q_here[None, None, :, None] + upper[:, None, None, None]]
  transfers between devices with their start and end apart: 2 -> 0, of which waited for: 0 -> 0; matrix products, arithmetic and copies ran while one was open for 17% -> 0% of each run, Pallas kernels for 0% -> 0%
where the time goes in v3:
time: 63.3 us; the launch traced here: 63.1 us
  Pallas kernels  57.7 us (91%)
  local copies, waits for them, and re-layouts  4.74 us (7%)
  between operations  0.64 us (1%)
    pallas_call x1, Pallas kernels, local(): pl.pallas_call(functools.partial(chain, legs, phys, block, chi * square *...  57.7 us
    unnamed x1, local copies, waits for them, and re-layouts  1.8 us
    reshape x2, local copies, waits for them, and re-layouts, local(): ket[0].transpose(2, 4, 3, 0, 1).reshape(square * phys, square)  1.75 us

profile of v3, /device:TPU:0, one launch (start us, length us, event | category | flops | bytes accessed | tf_op | source)
XLA Modules:
  0.0 63.1 jit_solution(15161216556062700235)
XLA Ops:
  0.6 1.0 %reshape.22 = bf16[72,36]{0,1:T(8,128)(2,1)S(1)} reshape(bf16[6,2,6,6,6]{2,1,0,4,3:T(2,128)(2,1)} %bitcast.31) | data formatting | bytes 10368 | tf_op jit(solution)/shard_map/reshape | solution.py:278
  1.7 0.7 %copy.18.ket_ref = bf16[72,36]{1,0:T(8,128)(2,1)} copy(bf16[72,36]{0,1:T(8,128)(2,1)S(1)} %reshape.22) | data formatting | bytes 10368 | tf_op jit(solution)/shard_map/reshape | solution.py:278
  2.4 57.7 %shard_map.158 = (bf16[36,48,96]{2,1,0:T(8,128)(2,1)}, f32[8,128]{1,0:T(8,128)}) custom-call(bf16[36,48,96]{2,1,0:T(8,128)(2,1)} %bitcast.27, bf16[36,48,96]{2,1,0:T(8,128)(2,1)} %bitcast.28, bf16[36,48,96]{2,1,0:T(8,128)(2,1)} %bitcast.29, bf16[72,36]{1,0:T(8,128)(2,1)} %copy.18.ket_ref, s32[1,96]{1,0:T(1,128)} %bond_ref.1, s32[1,96]{1,0:T(1,128)} %fresh_ref.1, ...), custom_call_target="tpu_custom_call" | custom-call | tf_op jit(solution)/shard_map/pallas_call | solution.py:288
  60.1 1.2 %slice.3 = f32[1,1]{1,0:T(1,128)} slice(f32[8,128]{1,0:T(8,128)} %get-tuple-element.5), slice={[0:1], [0:1]} | slice | bytes 8 | tf_op jit(solution)/shard_map/slice | solution.py:324
  61.3 1.8 %copy.20 = bf16[1,48,6,6,96]{4,1,3,2,0:T(8,128)(2,1)} copy(bf16[1,48,6,6,96]{4,1,3,2,0:T(8,128)(2,1)} %bitcast.30) | data formatting | bytes 663552

commit v4 on v3

--- a/solution.py
+++ b/solution.py
@@ -42,6 +42,10 @@
         at = lax.rem(me + k, total)
         return at, (at // secs, lax.rem(at, secs))
 
+    def close(k):
+        at = me_col * secs + lax.rem(me_sec + k, secs)
+        return lax.rem(at - me + total, total)
+
     def charge_copy():
         return pltpu.make_async_remote_copy(
             src_ref=charge_here, dst_ref=charge_next, send_sem=near_send.at[0], recv_sem=near_recv.at[0],
@@ -55,11 +59,18 @@
             device_id=(me_col, lax.rem(me_sec + k, secs)), device_id_type=MESH,
         )
 
-    def right_copy(t, source):
+    def right_copy():
         return pltpu.make_async_remote_copy(
-            src_ref=right_ref, dst_ref=right_all.at[source], send_sem=near_send.at[secs + t],
+            src_ref=right_ref, dst_ref=right_all.at[me_sec], send_sem=near_send.at[secs],
+            recv_sem=near_recv.at[1 + secs + me_sec],
+            device_id=(before, me_sec), device_id_type=MESH,
+        )
+
+    def right_pass(k, source):
+        return pltpu.make_async_remote_copy(
+            src_ref=right_all.at[source], dst_ref=right_all.at[source], send_sem=near_send.at[secs + k],
             recv_sem=near_recv.at[1 + secs + source],
-            device_id=(before, t), device_id_type=MESH,
+            device_id=(me_col, lax.rem(me_sec + k, secs)), device_id_type=MESH,
         )
 
     def down_rows(row):
@@ -90,8 +101,7 @@
         charge_copy().start()
         for k in range(1, secs):
             mps_copy(k, me_sec).start()
-        for t in range(secs):
-            right_copy(t, me_sec).start()
+        right_copy().start()
         charge_copy().wait_recv()
         after = charge_next[...].astype(F32)
         diff[...] = after[0:1] - down_rows(here[0:1])
@@ -127,6 +137,12 @@
             mps_copy(k, source).wait_recv()
             place(source, mps_all.at[source])
 
+    @pl.when(step == pl.num_programs(0) // 2)
+    def _():
+        right_copy().wait_recv()
+        for k in range(1, secs):
+            right_pass(k, me_sec).start()
+
     base = pl.multiple_of(step * (block * rows), block * rows)
     left = left_s[pl.ds(base, block * rows), :].astype(BF16)
     for u in range(legs):
@@ -149,7 +165,7 @@
         w2[:, i] = part.reshape(pairs * legs, slab, wide)
         return 0
 
-    lax.fori_loop(0, pairs * pairs, second, 0)
+    lax.fori_loop(0, pairs * pairs, second, 0, unroll=True)
 
     for dp in range(pairs):
         for r in range(legs):
@@ -168,8 +184,9 @@
         after = charge_next[...].astype(F32)
         diff[...] = down_rows(after[1:2]) - after[0:1]
         right_s[...] = jnp.zeros_like(right_s)
+        for k in range(1, secs):
+            right_pass(k, lax.rem(me_sec + k, secs)).wait_recv()
         for k in range(secs):
-            right_copy(k, k).wait_recv()
             delta = diff[k * half : (k + 1) * half, 0:chi]
             for r in range(legs):
                 for s in range(legs):
@@ -223,23 +240,36 @@
             return 0
 
         lax.fori_loop(1, total, send, 0)
-        lax.fori_loop(1, total, receive, 0)
-        lax.fori_loop(1, total, sent, 0)
-        charge_copy().wait_send()
-        for k in range(1, secs):
-            mps_copy(k, me_sec).wait_send()
-        for t in range(secs):
-            right_copy(t, me_sec).wait_send()
-        site = slots[me_col * secs]
-        for k in range(1, secs):
-            site = site + slots[me_col * secs + k]
+        site = jnp.broadcast_to(part, stage.shape)
+        for k in range(1, secs):
+            receive(close(k), 0)
+            site = site + slots[me_col * secs + lax.rem(me_sec + k, secs)]
         scale = lax.rsqrt(site[0:1, 0:1] / count + 1e-06)
-        sums = jnp.sum(slots[...].reshape(cols, secs, 8, LANES), axis=1) / count
-        log_ref[...] = jnp.sum(0.5 * jnp.log(sums + 1e-06), axis=0) / cols
         for d in range(legs):
             for e in range(legs):
                 values = image_s[pl.ds(d * PACK + e, half, stride=rows), :]
                 out_ref[d * legs + e] = (values * scale).astype(BF16)
+
+        def receive_far(k, _):
+            at, _where = other(k)
+
+            @pl.when(at // secs != me_col)
+            def _():
+                receive(k, 0)
+
+            return 0
+
+        lax.fori_loop(1, total, receive_far, 0)
+        sums = jnp.sum(slots[...].reshape(cols, secs, 1, LANES), axis=1) / count
+        logs = jnp.sum(0.5 * jnp.log(sums + 1e-06), axis=0) / cols
+        log_ref[...] = logs[0:1, 0:1]
+        lax.fori_loop(1, total, sent, 0)
+        charge_copy().wait_send()
+        for k in range(1, secs):
+            mps_copy(k, me_sec).wait_send()
+        right_copy().wait_send()
+        for k in range(1, secs):
+            right_pass(k, me_sec).wait_send()
 
 
 def picks(legs, phys):
@@ -267,7 +297,7 @@
     phys = ket.shape[5]
     pairs = legs // 2
     rows = legs * PACK
-    block = 8
+    block = 12
     wide = block * LANES
     square = legs * legs
     cols, secs = lax.axis_size("col"), lax.axis_size("sec")
@@ -284,7 +314,7 @@
     tables = picks(legs, phys)
     whole = lambda a: pl.BlockSpec(a.shape, lambda i: (0,) * len(a.shape))
     scalar = pl.BlockSpec(memory_space=pltpu.SMEM)
-    outs = [jax.ShapeDtypeStruct((square, half, chi), BF16), jax.ShapeDtypeStruct((8, LANES), F32)]
+    outs = [jax.ShapeDtypeStruct((square, half, chi), BF16), jax.ShapeDtypeStruct((1, 1), F32)]
     image, logs = pl.pallas_call(
         functools.partial(chain, legs, phys, block, chi * square * chi, cols, secs),
         grid=(half // block,),
@@ -306,8 +336,8 @@
             pltpu.VMEM((secs, square, half, chi), BF16),
             pltpu.VMEM((secs, square, half, chi), BF16),
             pltpu.VMEM((LANES, LANES), F32),
-            pltpu.VMEM((8, LANES), F32),
-            pltpu.VMEM((cols * secs, 8, LANES), F32),
+            pltpu.VMEM((1, LANES), F32),
+            pltpu.VMEM((cols * secs, 1, LANES), F32),
             pltpu.SemaphoreType.DMA((2 * secs,)),
             pltpu.SemaphoreType.DMA((1 + 2 * secs,)),
             pltpu.SemaphoreType.DMA((cols * secs,)),

time: 63.3 us -> 52.8 us (0.83)
  Pallas kernels: 57.7 us -> 46.5 us
  between operations: 0.64 us -> 2.44 us
  local copies, waits for them, and re-layouts: 4.74 us -> 3.55 us
    pallas_call x1, Pallas kernels: 57.7 us -> 46.5 us  [local(): pl.pallas_call(functools.partial(chain, legs, phys, block, chi * square *...]
    slice x1 -> x0, local copies, waits for them, and re-layouts: 1.19 us -> none  [local(): return (new_mps, logs[0, 0])]
where the time goes in v4:
time: 52.8 us; the launch traced here: 52.5 us
  Pallas kernels  46.5 us (88%)
  local copies, waits for them, and re-layouts  3.55 us (7%)
  between operations  2.44 us (5%)
    pallas_call x1, Pallas kernels, local(): pl.pallas_call(functools.partial(chain, legs, phys, block, chi * square *...  46.5 us
    unnamed x1, local copies, waits for them, and re-layouts  1.8 us
    reshape x2, local copies, waits for them, and re-layouts, local(): ket[0].transpose(2, 4, 3, 0, 1).reshape(square * phys, square)  1.75 us

profile of v4, /device:TPU:0, one launch (start us, length us, event | category | flops | bytes accessed | tf_op | source)
XLA Modules:
  0.0 52.5 jit_solution(8722407101217047647)
XLA Ops:
  0.6 1.0 %reshape.22 = bf16[72,36]{0,1:T(8,128)(2,1)S(1)} reshape(bf16[6,2,6,6,6]{2,1,0,4,3:T(2,128)(2,1)} %bitcast.31) | data formatting | bytes 10368 | tf_op jit(solution)/shard_map/reshape | solution.py:308
  1.7 0.7 %copy.18.ket_ref = bf16[72,36]{1,0:T(8,128)(2,1)} copy(bf16[72,36]{0,1:T(8,128)(2,1)S(1)} %reshape.22) | data formatting | bytes 10368 | tf_op jit(solution)/shard_map/reshape | solution.py:308
  2.4 46.5 %shard_map.158 = (bf16[36,48,96]{2,1,0:T(8,128)(2,1)}, f32[1,1]{1,0:T(1,128)}) custom-call(bf16[36,48,96]{2,1,0:T(8,128)(2,1)} %bitcast.27, bf16[36,48,96]{2,1,0:T(8,128)(2,1)} %bitcast.28, bf16[36,48,96]{2,1,0:T(8,128)(2,1)} %bitcast.29, bf16[72,36]{1,0:T(8,128)(2,1)} %copy.18.ket_ref, s32[1,96]{1,0:T(1,128)} %bond_ref.1, s32[1,96]{1,0:T(1,128)} %fresh_ref.1, ...), custom_call_target="tpu_custom_call" | custom-call | tf_op jit(solution)/shard_map/pallas_call | solution.py:318
  48.9 1.8 %copy.21 = bf16[1,48,6,6,96]{4,1,3,2,0:T(8,128)(2,1)} copy(bf16[1,48,6,6,96]{4,1,3,2,0:T(8,128)(2,1)} %bitcast.30) | data formatting | bytes 663552

commit v5 on v4

--- a/solution.py
+++ b/solution.py
@@ -203,7 +203,7 @@
             image_s[at, :] = image
             return square + jnp.sum((image * image).reshape(block * rows // 8, 8, chi), axis=0)
 
-        square = lax.fori_loop(0, half // block, last, jnp.zeros((8, chi), F32))
+        square = lax.fori_loop(0, half // block, last, jnp.zeros((8, chi), F32), unroll=True)
         part = jnp.sum(jnp.sum(square, axis=0, keepdims=True), axis=1, keepdims=True)
         stage[...] = jnp.broadcast_to(part, stage.shape)
         slots[me] = jnp.broadcast_to(part, stage.shape)

time: 52.8 us -> 52.1 us (0.987)
  Pallas kernels: 46.5 us -> 45.9 us
    pallas_call x1, Pallas kernels: 46.5 us -> 45.9 us  [local(): pl.pallas_call(functools.partial(chain, legs, phys, block, chi * square *...]
where the time goes in v5:
time: 52.1 us; the launch traced here: 51.9 us
  Pallas kernels  45.9 us (88%)
  local copies, waits for them, and re-layouts  3.55 us (7%)
  between operations  2.44 us (5%)
    pallas_call x1, Pallas kernels, local(): pl.pallas_call(functools.partial(chain, legs, phys, block, chi * square *...  45.9 us
    unnamed x1, local copies, waits for them, and re-layouts  1.8 us
    reshape x2, local copies, waits for them, and re-layouts, local(): ket[0].transpose(2, 4, 3, 0, 1).reshape(square * phys, square)  1.75 us

profile of v5, /device:TPU:0, one launch (start us, length us, event | category | flops | bytes accessed | tf_op | source)
XLA Modules:
  0.0 51.9 jit_solution(3057870471838500576)
XLA Ops:
  0.6 1.0 %reshape.22 = bf16[72,36]{0,1:T(8,128)(2,1)S(1)} reshape(bf16[6,2,6,6,6]{2,1,0,4,3:T(2,128)(2,1)} %bitcast.31) | data formatting | bytes 10368 | tf_op jit(solution)/shard_map/reshape | solution.py:308
  1.7 0.7 %copy.18.ket_ref = bf16[72,36]{1,0:T(8,128)(2,1)} copy(bf16[72,36]{0,1:T(8,128)(2,1)S(1)} %reshape.22) | data formatting | bytes 10368 | tf_op jit(solution)/shard_map/reshape | solution.py:308
  2.4 45.9 %shard_map.158 = (bf16[36,48,96]{2,1,0:T(8,128)(2,1)}, f32[1,1]{1,0:T(1,128)}) custom-call(bf16[36,48,96]{2,1,0:T(8,128)(2,1)} %bitcast.27, bf16[36,48,96]{2,1,0:T(8,128)(2,1)} %bitcast.28, bf16[36,48,96]{2,1,0:T(8,128)(2,1)} %bitcast.29, bf16[72,36]{1,0:T(8,128)(2,1)} %copy.18.ket_ref, s32[1,96]{1,0:T(1,128)} %bond_ref.1, s32[1,96]{1,0:T(1,128)} %fresh_ref.1, ...), custom_call_target="tpu_custom_call" | custom-call | tf_op jit(solution)/shard_map/pallas_call | solution.py:318
  48.3 1.8 %copy.21 = bf16[1,48,6,6,96]{4,1,3,2,0:T(8,128)(2,1)} copy(bf16[1,48,6,6,96]{4,1,3,2,0:T(8,128)(2,1)} %bitcast.30) | data formatting | bytes 663552
